TPU v7x, 128 devices: a whole 4x4x4 slice. The times are simulated.
128 devices in a mesh: view: 4 (over z_hi, core), depth: 32 (over z_lo, y, x).
Axes of the slice: x: 4, y: 4, z: 4 (z_hi: 2, z_lo: 2; z = z_hi * 2 + z_lo), core: 2. Of those that a mesh axis runs over, the one named last changes fastest.
Arguments:
- volume: float32 [512, 128, 2048], P(('view', 'depth')), may hold values from -6 to 6
- step_weights: float32 [4, 8, 64], P('view'), may hold values from -0.75 to 0.75
- row_interp: float32 [4, 64, 64], P('view'), may hold values from -0.75 to 0.75
- col_interp: float32 [4, 64, 64], P('view'), may hold values from -0.75 to 0.75
- tf_table: float32 [8, 8], replicated, may hold values from -3 to 3
- materials: int32 [8, 2, 32], P(None, None, 'depth'), may hold values from 0 to 7
- entry: int32 [4, 512, 128], P('view'), may hold values from 0 to 15
Outputs:
- picture: float32 [4, 3, 512, 128], P('view', None, 'depth')
All inputs are finite; a program needn't handle non-finite values.
Results may differ from a plain program's by a relative error of at most 0.00018.
Values sent between devices are 32-bit elements; how exact they have to be, the bound alone decides.
A program may use at most 64 MiB of HBM per device.

v0:
```python
import jax
import jax.numpy as jnp
from jax import lax
from jax.sharding import Mesh
from jax.sharding import PartitionSpec as P

DEPTH = ("depth_0", "depth_1", "depth_2")
VIEW_DEPTH = ("view", "depth_0", "depth_1", "depth_2")


def nothing_yet(shard, identity):
    return jnp.broadcast_to(jnp.asarray(identity, shard.dtype), shard.shape)


def carried_in(shard, axes, combine, identity):
    before = start = nothing_yet(shard, identity)
    total = shard
    for axis in reversed(axes):
        peers, index = (lax.axis_size(axis), lax.axis_index(axis))
        pieces = lax.all_gather(total, axis)
        inside, total = (start, start)
        for k in range(peers):
            passed = k < index
            total = combine(total, pieces[k])
            inside = jnp.where(passed, total, inside)
        before = combine(inside, before)
    return before


def in_blocks(shard, dim, peers):
    dims = shard.shape
    blocks = shard.reshape(*dims[:dim], peers, dims[dim] // peers, *dims[dim + 1 :])
    return jnp.moveaxis(blocks, dim, 0)


def summed_on_arrival(shard, axis, dim):
    peers = lax.axis_size(axis)
    blocks = lax.all_to_all(in_blocks(shard, dim, peers), axis, 0, 0, tiled=True)
    return jnp.sum(blocks, axis=0)


def finish_brick(first, rows_map, cols_map):
    highest = lax.Precision.HIGHEST
    edge = rows_map.shape[0]
    count_steps, total_rows, total_cols = first.shape
    second = first.reshape(count_steps, total_rows // edge, edge, total_cols)
    second = jnp.einsum("stky,rk->stry", second, rows_map, precision=highest)
    third = second.reshape(count_steps, total_rows, total_cols // edge, edge)
    third = jnp.einsum("szuj,cj->szuc", third, cols_map, precision=highest)
    return third.reshape(count_steps, total_rows, total_cols)


def expand_classes(classes, tf_table, edge):
    choices_range = jnp.arange(tf_table.shape[0], dtype=jnp.int32)
    onehot = (classes[:, :, None] == choices_range).astype(jnp.float32)
    tiles = jnp.einsum("abm,mc->cab", onehot, tf_table, precision=lax.Precision.HIGHEST)
    count_coef, tiles_rows, tiles_cols = tiles.shape
    spread = jnp.broadcast_to(
        tiles[:, :, None, :, None], (count_coef, tiles_rows, edge, tiles_cols, edge)
    )
    return spread.reshape(count_coef, tiles_rows * edge, tiles_cols * edge)


def shade(samples, coefficients, live_mask, step_length):
    emission = jax.nn.softplus(coefficients[0:3, None] * samples[None] + coefficients[3:6, None])
    tau = (
        step_length
        * live_mask[None]
        * jax.nn.softplus(coefficients[6][None] * samples + coefficients[7][None])
    )
    earlier = jnp.cumsum(tau, axis=0) - tau
    weights = jnp.exp(-earlier) * (1.0 - jnp.exp(-tau))
    colours = jnp.sum(weights[None] * emission, axis=1)
    passed = jnp.exp(-jnp.sum(tau, axis=0))
    return (colours, passed)


def multiply(earlier, later):
    return earlier * later


def shards(volume, step_weights, row_interp, col_interp, tf_table, materials, entry):
    view_count = lax.axis_size("view")
    depth_count = lax.axis_size(DEPTH)
    depth_index = lax.axis_index(DEPTH)
    planes, lateral, span_cells = volume.shape
    brick_edge = span_cells // depth_count
    all_weights = lax.all_gather(step_weights, "view", axis=0, tiled=True)
    count_steps = all_weights.shape[1]
    cells = volume.reshape(planes, lateral, depth_count, brick_edge)
    contracted = jnp.einsum("zybi,gsi->gbszy", cells, all_weights, precision=lax.Precision.HIGHEST)
    contracted = contracted.reshape(view_count * depth_count, count_steps, planes, lateral)
    received = lax.all_to_all(contracted, VIEW_DEPTH, split_axis=0, concat_axis=2, tiled=True)
    samples = finish_brick(received[0], row_interp[0], col_interp[0])
    coefficients = expand_classes(materials[:, :, 0], tf_table, brick_edge)
    live_mask = (entry[0] <= depth_index).astype(jnp.float32)
    step_length = 2.0 / (samples.shape[0] * depth_count)
    colours, passed = shade(samples, coefficients, live_mask, step_length)
    before = carried_in(passed, DEPTH, multiply, jnp.ones_like(passed))
    terms = before[None] * colours
    rows_part = summed_on_arrival(terms, DEPTH, 1)
    return rows_part[None]


def solution(mesh):
    torus = Mesh(
        mesh.devices.reshape(mesh.shape["view"], 2, 4, 4), ("view", "depth_0", "depth_1", "depth_2")
    )
    return jax.shard_map(
        shards,
        mesh=torus,
        in_specs=(
            P(VIEW_DEPTH, None, None),
            P("view", None, None),
            P("view", None, None),
            P("view", None, None),
            P(),
            P(None, None, DEPTH),
            P("view", None, None),
        ),
        out_specs=P("view", None, DEPTH, None),
        check_vma=False,
    )
```

profile of v0, /device:TPU:0, one launch (start us, length us, event | category | flops | bytes accessed | tf_op | source)
XLA Modules:
  0.0 162.9 jit_solution(9018118237173368795)
XLA Ops:
  6.5 5.4 %copy.64 = f32[4,128,2048]{1,2,0:T(8,128)} copy(f32[4,128,2048]{2,1,0:T(8,128)} %param.7) | data formatting | bytes 8388608 | tf_op args[0]
  11.9 7.2 %all_gather.15 = f32[4,8,64]{2,1,0:T(8,128)S(1)} all-gather(f32[1,8,64]{2,1,0:T(8,128)S(1)} %copy-done.6), channel_id=1, replica_groups=mesh['view'=4,'depth_0'=2,'depth_1'=4,'depth_2'=4] {'view'}, dimensions={0}, use_global_device_ids=true | all-gather | bytes 10240 | tf_op jit(solution)/shard_map/all_gather | solution.py:88
  19.1 3.9 %convolution_bitcast_fusion.1 = f32[4,32,8,4,128]{4,2,1,3,0:T(8,128)S(1)} fusion(f32[4,128,32,64,1]{1,3,2,0,4:T(8,128)} %bitcast.69, f32[4,8,64]{2,1,0:T(8,128)S(1)} %all_gather.15), kind=kOutput, calls=%fused_computation.13 | convolution fusion | flops 402653184 | bytes 6299648 | tf_op jit(solution)/shard_map/zybi,gsi->gbszy/dot_general | solution.py:91
  23.0 1.6 %copy.65 = f32[4,32,8,4,128]{4,2,3,1,0:T(8,128)} copy(f32[4,32,8,4,128]{4,2,1,3,0:T(8,128)S(1)} %convolution_bitcast_fusion.1) | data formatting | bytes 4194304 | tf_op jit(solution)/shard_map/zybi,gsi->gbszy/transpose | solution.py:91
  24.6 10.6 %all-to-all-start = ((f32[128,8,4,128]{3,1,2,0:T(8,128)}), f32[128,8,4,128]{3,1,2,0:T(8,128)S(1)}, u32[]{:S(2)}, u32[]{:S(2)}) async-start(f32[128,8,4,128]{3,1,2,0:T(8,128)} %bitcast.71), calls=%async_computation | async-start | bytes 4194304 | tf_op jit(solution)/shard_map/all_to_all | solution.py:93
  35.3 0.2 all-gather.3.cloned.1.call-start
  35.7 0.2 convolution_bitcast_fusion.2
  36.3 28.8 %all-to-all-done = f32[128,8,4,128]{3,1,2,0:T(8,128)S(1)} async-done(((f32[128,8,4,128]{3,1,2,0:T(8,128)}), f32[128,8,4,128]{3,1,2,0:T(8,128)S(1)}, u32[]{:S(2)}, u32[]{:S(2)}) %all-to-all-start) | async-done | bytes 2097184 | tf_op jit(solution)/shard_map/all_to_all | solution.py:93
  65.0 0.5 copy.66
  65.6 0.2 copy-done.5
  65.8 2.0 %convolution_bitcast_fusion = f32[8,8,64,128]{3,2,1,0:T(8,128)S(1)} fusion(f32[8,8,64,128]{3,2,1,0:T(8,128)S(1)} %bitcast.72, f32[1,64,64]{2,1,0:T(8,128)S(1)} %copy-done.5), kind=kOutput, calls=%fused_computation.12 | convolution fusion | flops 402653184 | bytes 4210688 | tf_op jit(solution)/shard_map/stky,rk->stry/dot_general | solution.py:47
  67.8 3.7 %reshape.111 = f32[8,512,2,64]{3,2,1,0:T(2,128)} reshape(f32[8,8,64,128]{3,2,1,0:T(8,128)S(1)} %convolution_bitcast_fusion) | data formatting | bytes 4194304 | tf_op jit(solution)/shard_map/reshape | solution.py:48
  71.5 7.0 %fusion.10 = (u8[512,2,64]{0,2,1:T(8,128)(4,1)S(1)}, f32[8,512,2,64]{1,3,2,0:T(8,128)S(1)}) fusion(f32[512,2]{0,1:T(2,128)S(1)} %broadcast_in_dim.39, f32[512,2]{0,1:T(2,128)S(1)} %broadcast_in_dim.37, f32[1,64,64]{2,1,0:T(8,128)S(1)} %copy-done, f32[8,512,2,64]{3,2,1,0:T(2,128)} %reshape.111), kind=kOutput, calls=%fused_computation.20 | convolution fusion | flops 406257664 | bytes 4284416 | tf_op jit(solution)/shard_map/szuj,cj->szuc/dot_general | solution.py:49
  78.5 1.4 multiply_reduce_fusion
  80.0 0.8 copy.68
  80.9 0.3 all-gather.5.cloned.1.call-start
  81.2 20.0 %all-gather.3.cloned.1.call-done = f32[4,512,128]{2,1,0:T(8,128)} async-done(((f32[1,512,128]{2,1,0:T(8,128)}), f32[4,512,128]{2,1,0:T(8,128)}) %all-gather.3.cloned.1.call-update) | async-done | bytes 1048592 | tf_op jit(solution)/shard_map/all_gather | solution.py:20
  101.1 1.9 %slice_multiply_fusion.4 = f32[1,512,128]{2,1,0:T(8,128)} fusion(f32[4,512,128]{2,1,0:T(8,128)} %all-gather.3.cloned.1.call-done), kind=kLoop, calls=%fused_computation.27 | loop fusion | flops 196608 | bytes 1310720 | tf_op jit(solution)/shard_map/mul | solution.py:79
  103.2 0.1 broadcast_in_dim.42
  103.7 1.6 %broadcast_in_dim.46 = f32[3,8,64,2,64]{4,3,2,1,0:T(2,128)} broadcast(f32[3,8,2]{2,1,0:T(8,128)S(1)} %copy.72), dimensions={0,1,3} | broadcast | bytes 786624 | tf_op jit(solution)/shard_map/broadcast_in_dim | solution.py:58
  105.4 3.1 %add.64 = f32[3,512,128]{2,1,0:T(8,128)} reshape(f32[3,8,64,2,64]{4,3,2,1,0:T(2,128)} %broadcast_in_dim.46) | data formatting | bytes 1572864 | tf_op jit(solution)/shard_map/add | solution.py:65
  108.5 1.6 %broadcast_in_dim.45 = f32[3,8,64,2,64]{4,3,2,1,0:T(2,128)} broadcast(f32[3,8,2]{2,1,0:T(8,128)S(1)} %copy.70), dimensions={0,1,3} | broadcast | bytes 786624 | tf_op jit(solution)/shard_map/broadcast_in_dim | solution.py:58
  110.2 3.0 %mul.170 = f32[3,512,128]{2,1,0:T(8,128)} reshape(f32[3,8,64,2,64]{4,3,2,1,0:T(2,128)} %broadcast_in_dim.45) | data formatting | bytes 1572864 | tf_op jit(solution)/shard_map/mul | solution.py:65
  113.2 1.8 %copy.71 = f32[8,512,128]{2,1,0:T(8,128)} copy(f32[8,512,128]{1,2,0:T(8,128)S(1)} %bitcast.67) | data formatting | bytes 4194304 | tf_op jit(solution)/shard_map/reshape | solution.py:50
  115.0 4.2 %subtract_multiply_fusion = f32[8,512,128]{1,2,0:T(8,128)} fusion(f32[8,512,128]{1,2,0:T(8,128)S(1)} %bitcast.68, f32[512,128]{0,1:T(8,128)S(1)} %broadcast_in_dim.44, f32[512,128]{0,1:T(8,128)S(1)} %broadcast_in_dim.42, f32[512,128]{0,1:T(8,128)S(1)} %fusion.23), kind=kOutput, calls=%fused_computation.9 | output fusion | flops 15728640 | bytes 4980736 | tf_op jit(solution)/shard_map/jit(cumsum)/reduce_window_sum | solution.py:71
  119.2 3.1 %copy.69 = f32[8,512,128]{2,1,0:T(8,128)} copy(f32[8,512,128]{1,2,0:T(8,128)} %subtract_multiply_fusion) | data formatting | bytes 4194304 | tf_op jit(solution)/shard_map/mul | solution.py:72
  122.3 5.7 %fusion.1 = f32[3,512,128]{2,1,0:T(8,128)S(1)} fusion(f32[3,512,128]{2,1,0:T(8,128)} %add.64, f32[8,512,128]{2,1,0:T(8,128)S(1)} %copy-done.1, f32[3,512,128]{2,1,0:T(8,128)} %mul.170, f32[8,512,128]{2,1,0:T(8,128)} %copy.69), kind=kLoop, calls=%fused_computation.2 | loop fusion | flops 15532032 | bytes 6553600 | tf_op jit(solution)/shard_map/reduce_sum | solution.py:73
  128.0 1.4 slice_multiply_fusion.1
  129.4 7.0 %all_gather.18 = f32[2,512,128]{2,1,0:T(8,128)S(1)} all-gather(f32[1,512,128]{2,1,0:T(8,128)S(1)} %slice_multiply_fusion.1), channel_id=1, replica_groups=mesh['view'=4,'depth_0'=2,'depth_1'=4,'depth_2'=4] {'depth_0'}, dimensions={0}, use_global_device_ids=true | all-gather | bytes 786432 | tf_op jit(solution)/shard_map/all_gather | solution.py:20
  136.5 0.2 fusion.12
  136.8 18.6 %all_to_all.20 = f32[32,3,16,128]{3,2,1,0:T(8,128)S(1)} all-to-all(f32[32,3,16,128]{3,2,1,0:T(8,128)S(1)} %copy.73), channel_id=1, replica_groups=mesh['view'=4,'depth_0'=2,'depth_1'=4,'depth_2'=4] {'depth_0','depth_1',..., dimensions={0} | all-to-all | bytes 1572864 | tf_op jit(solution)/shard_map/all_to_all | solution.py:38
  155.4 0.7 reduce_sum.32
  (37 shorter events, 1.3 us)
Async XLA Ops:
  6.5 65.0 %copy-start = (f32[1,64,64]{2,1,0:T(8,128)S(1)}, f32[1,64,64]{2,1,0:T(8,128)}, u32[]{:S(2)}) copy-start(f32[1,64,64]{2,1,0:T(8,128)} %param.10) | copy-start | bytes 49156
  6.5 5.4 %copy-start.6 = (f32[1,8,64]{2,1,0:T(8,128)S(1)}, f32[1,8,64]{2,1,0:T(8,128)}, u32[]{:S(2)}) copy-start(f32[1,8,64]{2,1,0:T(8,128)} %param.8) | copy-start | bytes 6148
  24.6 10.9 %copy-start.4 = (s32[1,512,128]{2,1,0:T(8,128)S(1)}, s32[1,512,128]{2,1,0:T(8,128)}, u32[]{:S(2)}) copy-start(s32[1,512,128]{2,1,0:T(8,128)} %param.13) | copy-start | bytes 786436
  24.6 11.0 %copy-start.7 = (f32[8,8]{1,0:T(8,128)S(1)}, f32[8,8]{1,0:T(8,128)}, u32[]{:S(2)}) copy-start(f32[8,8]{1,0:T(8,128)} %param.11) | copy-start | bytes 772
  24.6 11.0 %copy-start.8 = (s32[8,2,1]{0,2,1:T(1,128)S(1)}, s32[8,2,1]{0,2,1:T(1,128)}, u32[]{:S(2)}) copy-start(s32[8,2,1]{0,2,1:T(1,128)} %param.12) | copy-start | bytes 196
  24.6 40.4 %all-to-all-start = ((f32[128,8,4,128]{3,1,2,0:T(8,128)}), f32[128,8,4,128]{3,1,2,0:T(8,128)S(1)}, u32[]{:S(2)}, u32[]{:S(2)}) async-start(f32[128,8,4,128]{3,1,2,0:T(8,128)} %bitcast.71), calls=%async_computation | async-start | bytes 4194304 | tf_op jit(solution)/shard_map/all_to_all | solution.py:93
  35.3 65.9 %all-gather.3.cloned.1.call-start = ((), (), s32[]{:S(2)}) async-start(), calls=%async_computation.2 | async-start | bytes 1310720 | tf_op jit(solution)/shard_map/all_gather | solution.py:20
  65.0 0.8 copy-start.5
  80.9 47.1 %all-gather.5.cloned.1.call-start = ((), (), s32[]{:S(2)}) async-start(), calls=%async_computation.3 | async-start | bytes 1310720 | tf_op jit(solution)/shard_map/all_gather | solution.py:20
  119.2 3.1 %copy-start.1 = (f32[8,512,128]{2,1,0:T(8,128)S(1)}, f32[8,512,128]{2,1,0:T(8,128)}, u32[]{:S(2)}) copy-start(f32[8,512,128]{2,1,0:T(8,128)} %copy.71) | copy-start | bytes 6291460
  128.0 8.5 %copy-start.2 = (f32[4,512,128]{2,1,0:T(8,128)S(1)}, f32[4,512,128]{2,1,0:T(8,128)}, u32[]{:S(2)}) copy-start(f32[4,512,128]{2,1,0:T(8,128)} %all-gather.3.cloned.1.call-done) | copy-start | bytes 3145732
  128.0 8.4 %copy-start.3 = (f32[4,512,128]{2,1,0:T(8,128)S(1)}, f32[4,512,128]{2,1,0:T(8,128)}, u32[]{:S(2)}) copy-start(f32[4,512,128]{2,1,0:T(8,128)} %all-gather.5.cloned.1.call-done) | copy-start | bytes 3145732
Sparse Core Ops, SparseCore 0:
  81.0 20.0 all-gather.2
  103.2 24.4 all-gather.4
where the time goes:
time: 163 us
  waiting for transfers between devices  48.8 us (30%)
  blocking collectives  32.9 us (20%)
  local copies, waits for them, and re-layouts  27.7 us (17%)
  other arithmetic  15.6 us (10%)
  between operations  13.6 us (8%)
  matrix products  13.1 us (8%)
  starting transfers between devices  11.1 us (7%)
    all_to_all x1, waiting for transfers between devices, shards(): lax.all_to_all(contracted, VIEW_DEPTH, split_axis=0, concat_axis=2, tiled...  28.8 us
    all_gather x2, waiting for transfers between devices, carried_in(): pieces = lax.all_gather(total, axis)  20 us
    all_to_all x1, blocking collectives, summed_on_arrival(): lax.all_to_all(in_blocks(shard, dim, peers), axis, 0, 0, tiled=True)  18.6 us
    all_to_all x1, starting transfers between devices, shards(): lax.all_to_all(contracted, VIEW_DEPTH, split_axis=0, concat_axis=2, tiled...  10.6 us
    all_gather x1, blocking collectives, shards(): all_weights = lax.all_gather(step_weights, 'view', axis=0, tiled=True)  7.25 us
    dot_general x1, matrix products, finish_brick(): third = jnp.einsum('szuj,cj->szuc', third, cols_map, precision=highest)  7.04 us
    all_gather x1, blocking collectives, carried_in(): pieces = lax.all_gather(total, axis)  7.04 us
    unnamed x20, local copies, waits for them, and re-layouts  5.73 us
  transfers between devices with their start and end apart: 3, of which 2 were waited for; matrix products, arithmetic and copies ran while one was open for 16% of the time, Pallas kernels for 0%

commit v1 on v0

--- a/solution.py
+++ b/solution.py
@@ -6,6 +6,13 @@
 
 DEPTH = ("depth_0", "depth_1", "depth_2")
 VIEW_DEPTH = ("view", "depth_0", "depth_1", "depth_2")
+
+
+def swapped_in(x, mesh_axis, d):
+    peers = lax.axis_size(mesh_axis)
+    pieces = jnp.stack([x for _ in range(peers)])
+    pieces = lax.all_to_all(pieces, mesh_axis, split_axis=0, concat_axis=0)
+    return jnp.concatenate(pieces, axis=d)
 
 
 def nothing_yet(shard, identity):
@@ -85,7 +92,7 @@
     depth_index = lax.axis_index(DEPTH)
     planes, lateral, span_cells = volume.shape
     brick_edge = span_cells // depth_count
-    all_weights = lax.all_gather(step_weights, "view", axis=0, tiled=True)
+    all_weights = swapped_in(step_weights, "view", 0)
     count_steps = all_weights.shape[1]
     cells = volume.reshape(planes, lateral, depth_count, brick_edge)
     contracted = jnp.einsum("zybi,gsi->gbszy", cells, all_weights, precision=lax.Precision.HIGHEST)

time: 163 us -> 164 us (level)
  blocking collectives: 32.9 us -> 25.7 us
  starting transfers between devices: 11.1 us -> 16.5 us
  local copies, waits for them, and re-layouts: 27.7 us -> 29.7 us
    all_gather x1 -> x0, blocking collectives: 7.25 us -> none  [shards(): all_weights = lax.all_gather(step_weights, 'view', axis=0, tiled=True)]
    all_to_all x0 -> x1, starting transfers between devices: none -> 5.26 us  [swapped_in(): pieces = lax.all_to_all(pieces, mesh_axis, split_axis=0, concat_axis=0)]
  transfers between devices with their start and end apart: 3 -> 4, of which waited for: 2 -> 2; matrix products, arithmetic and copies ran while one was open for 16% -> 19% of each run, Pallas kernels for 0% -> 0%
where the time goes in v1:
time: 164 us
  waiting for transfers between devices  48.8 us (30%)
  local copies, waits for them, and re-layouts  29.7 us (18%)
  blocking collectives  25.7 us (16%)
  starting transfers between devices  16.5 us (10%)
  other arithmetic  16.3 us (10%)
  between operations  13.6 us (8%)
  matrix products  13.1 us (8%)
    all_to_all x1, waiting for transfers between devices, shards(): lax.all_to_all(contracted, VIEW_DEPTH, split_axis=0, concat_axis=2, tiled...  28.8 us
    all_gather x2, waiting for transfers between devices, carried_in(): pieces = lax.all_gather(total, axis)  20 us
    all_to_all x1, blocking collectives, summed_on_arrival(): lax.all_to_all(in_blocks(shard, dim, peers), axis, 0, 0, tiled=True)  18.6 us
    all_to_all x1, starting transfers between devices, shards(): lax.all_to_all(contracted, VIEW_DEPTH, split_axis=0, concat_axis=2, tiled...  10.7 us
    all_gather x1, blocking collectives, carried_in(): pieces = lax.all_gather(total, axis)  7.04 us
    dot_general x1, matrix products, finish_brick(): third = jnp.einsum('szuj,cj->szuc', third, cols_map, precision=highest)  7.04 us
    unnamed x20, local copies, waits for them, and re-layouts  6.51 us
    reduce_sum x1, other arithmetic, shade(): colours = jnp.sum(weights[None] * emission, axis=1)  5.66 us
  transfers between devices with their start and end apart: 4, of which 2 were waited for; matrix products, arithmetic and copies ran while one was open for 19% of the time, Pallas kernels for 0%

profile of v1, /device:TPU:0, one launch (start us, length us, event | category | flops | bytes accessed | tf_op | source)
XLA Modules:
  0.0 163.7 jit_solution(14250828601573525158)
XLA Ops:
  6.5 0.7 stack.2
  7.2 0.7 reshape.119
  7.9 5.3 %all-to-all-start = ((f32[4,1,512]{2,1,0:T(1,128)}), f32[4,1,512]{2,1,0:T(1,128)S(1)}, u32[]{:S(2)}, u32[]{:S(2)}) async-start(f32[4,1,512]{2,1,0:T(1,128)} %reshape.119), calls=%async_computation | async-start | bytes 16384 | tf_op jit(solution)/shard_map/all_to_all | solution.py:14
  13.2 5.4 %copy.64 = f32[4,128,2048]{1,2,0:T(8,128)} copy(f32[4,128,2048]{2,1,0:T(8,128)} %param.7) | data formatting | bytes 8388608 | tf_op args[0]
  18.6 0.5 broadcast.86
  19.1 0.7 reduce.3
  19.8 3.9 %convolution_bitcast_fusion.1 = f32[4,32,8,4,128]{4,2,1,3,0:T(8,128)S(1)} fusion(f32[4,128,32,64,1]{1,3,2,0,4:T(8,128)} %bitcast.72, f32[4,1,8,64]{3,2,1,0:T(8,128)S(1)} %reshape.120), kind=kOutput, calls=%fused_computation.13 | convolution fusion | flops 402653184 | bytes 6299648 | tf_op jit(solution)/shard_map/zybi,gsi->gbszy/dot_general | solution.py:98
  23.7 1.6 copy.65
  25.3 10.7 %all-to-all-start.1 = ((f32[128,8,4,128]{3,1,2,0:T(8,128)}), f32[128,8,4,128]{3,1,2,0:T(8,128)S(1)}, u32[]{:S(2)}, u32[]{:S(2)}) async-start(f32[128,8,4,128]{3,1,2,0:T(8,128)} %bitcast.74), calls=%async_computation.1 | async-start | bytes 4194304 | tf_op jit(solution)/shard_map/all_to_all | solution.py:100
  36.0 0.2 all-gather.3.cloned.1.call-start
  37.0 28.8 %all-to-all-done.1 = f32[128,8,4,128]{3,1,2,0:T(8,128)S(1)} async-done(((f32[128,8,4,128]{3,1,2,0:T(8,128)}), f32[128,8,4,128]{3,1,2,0:T(8,128)S(1)}, u32[]{:S(2)}, u32[]{:S(2)}) %all-to-all-start.1) | async-done | bytes 2097184 | tf_op jit(solution)/shard_map/all_to_all | solution.py:100
  65.8 0.5 copy.66
  66.6 2.0 %convolution_bitcast_fusion = f32[8,8,64,128]{3,2,1,0:T(8,128)S(1)} fusion(f32[8,8,64,128]{3,2,1,0:T(8,128)S(1)} %bitcast.75, f32[1,64,64]{2,1,0:T(8,128)S(1)} %copy-done.5), kind=kOutput, calls=%fused_computation.12 | convolution fusion | flops 402653184 | bytes 4210688 | tf_op jit(solution)/shard_map/stky,rk->stry/dot_general | solution.py:54
  68.6 3.7 %reshape.118 = f32[8,512,2,64]{3,2,1,0:T(2,128)} reshape(f32[8,8,64,128]{3,2,1,0:T(8,128)S(1)} %convolution_bitcast_fusion) | data formatting | bytes 4194304 | tf_op jit(solution)/shard_map/reshape | solution.py:55
  72.3 7.0 %fusion.10 = (u8[512,2,64]{0,2,1:T(8,128)(4,1)S(1)}, f32[8,512,2,64]{1,3,2,0:T(8,128)S(1)}) fusion(f32[512,2]{0,1:T(2,128)S(1)} %broadcast_in_dim.39, f32[512,2]{0,1:T(2,128)S(1)} %broadcast_in_dim.37, f32[1,64,64]{2,1,0:T(8,128)S(1)} %copy-done, f32[8,512,2,64]{3,2,1,0:T(2,128)} %reshape.118), kind=kOutput, calls=%fused_computation.20 | convolution fusion | flops 406257664 | bytes 4284416 | tf_op jit(solution)/shard_map/szuj,cj->szuc/dot_general | solution.py:56
  79.3 1.4 multiply_reduce_fusion
  80.8 0.8 copy.68
  81.7 0.3 all-gather.5.cloned.1.call-start
  81.9 20.0 %all-gather.3.cloned.1.call-done = f32[4,512,128]{2,1,0:T(8,128)} async-done(((f32[1,512,128]{2,1,0:T(8,128)}), f32[4,512,128]{2,1,0:T(8,128)}) %all-gather.3.cloned.1.call-update) | async-done | bytes 1048592 | tf_op jit(solution)/shard_map/all_gather | solution.py:27
  101.9 1.9 %slice_multiply_fusion.4 = f32[1,512,128]{2,1,0:T(8,128)} fusion(f32[4,512,128]{2,1,0:T(8,128)} %all-gather.3.cloned.1.call-done), kind=kLoop, calls=%fused_computation.27 | loop fusion | flops 196608 | bytes 1310720 | tf_op jit(solution)/shard_map/mul | solution.py:86
  104.5 1.6 %broadcast_in_dim.46 = f32[3,8,64,2,64]{4,3,2,1,0:T(2,128)} broadcast(f32[3,8,2]{2,1,0:T(8,128)S(1)} %copy.72), dimensions={0,1,3} | broadcast | bytes 786624 | tf_op jit(solution)/shard_map/broadcast_in_dim | solution.py:65
  106.1 3.1 %add.64 = f32[3,512,128]{2,1,0:T(8,128)} reshape(f32[3,8,64,2,64]{4,3,2,1,0:T(2,128)} %broadcast_in_dim.46) | data formatting | bytes 1572864 | tf_op jit(solution)/shard_map/add | solution.py:72
  109.3 1.6 %broadcast_in_dim.45 = f32[3,8,64,2,64]{4,3,2,1,0:T(2,128)} broadcast(f32[3,8,2]{2,1,0:T(8,128)S(1)} %copy.70), dimensions={0,1,3} | broadcast | bytes 786624 | tf_op jit(solution)/shard_map/broadcast_in_dim | solution.py:65
  111.0 3.0 %mul.170 = f32[3,512,128]{2,1,0:T(8,128)} reshape(f32[3,8,64,2,64]{4,3,2,1,0:T(2,128)} %broadcast_in_dim.45) | data formatting | bytes 1572864 | tf_op jit(solution)/shard_map/mul | solution.py:72
  114.0 1.8 %copy.71 = f32[8,512,128]{2,1,0:T(8,128)} copy(f32[8,512,128]{1,2,0:T(8,128)S(1)} %bitcast.70) | data formatting | bytes 4194304 | tf_op jit(solution)/shard_map/reshape | solution.py:57
  115.8 4.2 %subtract_multiply_fusion = f32[8,512,128]{1,2,0:T(8,128)} fusion(f32[8,512,128]{1,2,0:T(8,128)S(1)} %bitcast.71, f32[512,128]{0,1:T(8,128)S(1)} %broadcast_in_dim.44, f32[512,128]{0,1:T(8,128)S(1)} %broadcast_in_dim.42, f32[512,128]{0,1:T(8,128)S(1)} %fusion.23), kind=kOutput, calls=%fused_computation.9 | output fusion | flops 15728640 | bytes 4980736 | tf_op jit(solution)/shard_map/jit(cumsum)/reduce_window_sum | solution.py:78
  120.0 3.1 %copy.69 = f32[8,512,128]{2,1,0:T(8,128)} copy(f32[8,512,128]{1,2,0:T(8,128)} %subtract_multiply_fusion) | data formatting | bytes 4194304 | tf_op jit(solution)/shard_map/mul | solution.py:79
  123.1 5.7 %fusion.1 = f32[3,512,128]{2,1,0:T(8,128)S(1)} fusion(f32[3,512,128]{2,1,0:T(8,128)} %add.64, f32[8,512,128]{2,1,0:T(8,128)S(1)} %copy-done.1, f32[3,512,128]{2,1,0:T(8,128)} %mul.170, f32[8,512,128]{2,1,0:T(8,128)} %copy.69), kind=kLoop, calls=%fused_computation.2 | loop fusion | flops 15532032 | bytes 6553600 | tf_op jit(solution)/shard_map/reduce_sum | solution.py:80
  128.8 1.4 slice_multiply_fusion.1
  130.2 7.0 %all_gather.14 = f32[2,512,128]{2,1,0:T(8,128)S(1)} all-gather(f32[1,512,128]{2,1,0:T(8,128)S(1)} %slice_multiply_fusion.1), channel_id=1, replica_groups=mesh['view'=4,'depth_0'=2,'depth_1'=4,'depth_2'=4] {'depth_0'}, dimensions={0}, use_global_device_ids=true | all-gather | bytes 786432 | tf_op jit(solution)/shard_map/all_gather | solution.py:27
  137.6 18.6 %all_to_all.25 = f32[32,3,16,128]{3,2,1,0:T(8,128)S(1)} all-to-all(f32[32,3,16,128]{3,2,1,0:T(8,128)S(1)} %copy.73), channel_id=1, replica_groups=mesh['view'=4,'depth_0'=2,'depth_1'=4,'depth_2'=4] {'depth_0','depth_1',..., dimensions={0} | all-to-all | bytes 1572864 | tf_op jit(solution)/shard_map/all_to_all | solution.py:45
  156.2 0.7 reduce_sum.32
  (41 shorter events, 2.1 us)
Async XLA Ops:
  6.5 65.7 %copy-start = (f32[1,64,64]{2,1,0:T(8,128)S(1)}, f32[1,64,64]{2,1,0:T(8,128)}, u32[]{:S(2)}) copy-start(f32[1,64,64]{2,1,0:T(8,128)} %param.10) | copy-start | bytes 49156
  7.9 10.6 %all-to-all-start = ((f32[4,1,512]{2,1,0:T(1,128)}), f32[4,1,512]{2,1,0:T(1,128)S(1)}, u32[]{:S(2)}, u32[]{:S(2)}) async-start(f32[4,1,512]{2,1,0:T(1,128)} %reshape.119), calls=%async_computation | async-start | bytes 16384 | tf_op jit(solution)/shard_map/all_to_all | solution.py:14
  25.3 11.0 %copy-start.4 = (s32[1,512,128]{2,1,0:T(8,128)S(1)}, s32[1,512,128]{2,1,0:T(8,128)}, u32[]{:S(2)}) copy-start(s32[1,512,128]{2,1,0:T(8,128)} %param.13) | copy-start | bytes 786436
  25.3 11.1 %copy-start.6 = (f32[8,8]{1,0:T(8,128)S(1)}, f32[8,8]{1,0:T(8,128)}, u32[]{:S(2)}) copy-start(f32[8,8]{1,0:T(8,128)} %param.11) | copy-start | bytes 772
  25.3 11.1 %copy-start.7 = (s32[8,2,1]{0,2,1:T(1,128)S(1)}, s32[8,2,1]{0,2,1:T(1,128)}, u32[]{:S(2)}) copy-start(s32[8,2,1]{0,2,1:T(1,128)} %param.12) | copy-start | bytes 196
  25.3 40.5 %all-to-all-start.1 = ((f32[128,8,4,128]{3,1,2,0:T(8,128)}), f32[128,8,4,128]{3,1,2,0:T(8,128)S(1)}, u32[]{:S(2)}, u32[]{:S(2)}) async-start(f32[128,8,4,128]{3,1,2,0:T(8,128)} %bitcast.74), calls=%async_computation.1 | async-start | bytes 4194304 | tf_op jit(solution)/shard_map/all_to_all | solution.py:100
  36.0 65.9 %all-gather.3.cloned.1.call-start = ((), (), s32[]{:S(2)}) async-start(), calls=%async_computation.3 | async-start | bytes 1310720 | tf_op jit(solution)/shard_map/all_gather | solution.py:27
  65.8 0.8 copy-start.5
  81.7 47.2 %all-gather.5.cloned.1.call-start = ((), (), s32[]{:S(2)}) async-start(), calls=%async_computation.4 | async-start | bytes 1310720 | tf_op jit(solution)/shard_map/all_gather | solution.py:27
  120.0 3.1 %copy-start.1 = (f32[8,512,128]{2,1,0:T(8,128)S(1)}, f32[8,512,128]{2,1,0:T(8,128)}, u32[]{:S(2)}) copy-start(f32[8,512,128]{2,1,0:T(8,128)} %copy.71) | copy-start | bytes 6291460
  128.8 8.5 %copy-start.2 = (f32[4,512,128]{2,1,0:T(8,128)S(1)}, f32[4,512,128]{2,1,0:T(8,128)}, u32[]{:S(2)}) copy-start(f32[4,512,128]{2,1,0:T(8,128)} %all-gather.3.cloned.1.call-done) | copy-start | bytes 3145732
  128.8 8.4 %copy-start.3 = (f32[4,512,128]{2,1,0:T(8,128)S(1)}, f32[4,512,128]{2,1,0:T(8,128)}, u32[]{:S(2)}) copy-start(f32[4,512,128]{2,1,0:T(8,128)} %all-gather.5.cloned.1.call-done) | copy-start | bytes 3145732
Sparse Core Ops, SparseCore 0:
  81.8 20.0 all-gather.2
  104.0 24.4 all-gather.4
